TPU v7x, 256 devices: a whole 4x4x8 slice. The times are simulated.
256 devices in a mesh: gx: 16 (over x, z_lo, core), gy: 16 (over y, z_hi).
Axes of the slice: x: 4, y: 4, z: 8 (z_hi: 4, z_lo: 2; z = z_hi * 2 + z_lo), core: 2. Of those that a mesh axis runs over, the one named last changes fastest.
Arguments:
- tokens: bfloat16 [131072, 1280], P(('gx', 'gy')), may hold values from -6 to 6
- out_grad: bfloat16 [131072, 1280], P(('gx', 'gy')), may hold values from -400 to 400
- segments: int32 [256, 512], P(('gx', 'gy')), may hold values from 0 to 7, never falling along the last dimension, each value on 1 to 256 neighbouring positions
- pos_rows: int32 [131072], P(('gx', 'gy')), may hold values from 0 to 15
- pos_cols: int32 [131072], P(('gx', 'gy')), may hold values from 0 to 15
- row_table: bfloat16 [16, 1280], replicated, may hold values from -4 to 4
- col_table: bfloat16 [16, 1280], replicated, may hold values from -4 to 4
- norm_gain: float32 [1280], replicated, may hold values from 0.25 to 1.75
- master_up: float32 [1280, 2560], P('gx'), may hold values from -0.15625 to 0.15625
- master_down: float32 [1280, 2560], P('gx'), may hold values from -0.125 to 0.125
- moment_up: float32 [1280, 2560], P('gx'), may hold values from -6 to 6
- moment_down: float32 [1280, 2560], P('gx'), may hold values from -6 to 6
Outputs:
- new_master_up: float32 [1280, 2560], P('gx')
- new_master_down: float32 [1280, 2560], P('gx')
- new_moment_up: float32 [1280, 2560], P('gx')
- new_moment_down: float32 [1280, 2560], P('gx')
Inputs may be any that keep to these rules, and one draw needn't show every extreme that they name: `segments`: each replica's 512 tokens hold all 8 images in order, each of 1 to 256 tokens.
All inputs are finite; a program needn't handle non-finite values.
Results may differ from a plain program's by a relative error of at most 0.02.
Values may be sent and summed in bfloat16 or wider, within the bound.
No kernel may reach another device: no remote copies, remote signals or barrier semaphores. Data moves between devices by JAX's collectives and lax.ppermute only.
A program may use at most 128 MiB of HBM per device.

v0:
```python
import jax
import jax.numpy as jnp
from jax import lax
from jax.sharding import Mesh
from jax.sharding import PartitionSpec as P

D = 1280
FF = 2560
GRID = 16
IMGS = 8
GX = ("gx_0", "gx_1", "gx_2")
GY = ("gy_0", "gy_1")
GX_GY = ("gx_0", "gx_1", "gx_2", "gy_0", "gy_1")
momentum_keep = 0.9
learn_rate = 0.01


def in_blocks(value, dim, size):
    lengths = value.shape
    pieces = value.reshape(*lengths[:dim], size, lengths[dim] // size, *lengths[dim + 1 :])
    return jnp.moveaxis(pieces, dim, 0)


def sent_and_summed(value, axis, dim):
    size = lax.axis_size(axis)
    pieces = lax.all_to_all(in_blocks(value, dim, size), axis, 0, 0, tiled=True)
    return jnp.sum(pieces.astype(jnp.float32), axis=0)


def over_axes(value, axes):
    for axis in axes:
        value = lax.psum(value, axis)
    return value


def gather_turned(arrays, axis, dims):
    turned = [jnp.moveaxis(a, dim, 0) for a, dim in zip(arrays, dims)]
    widths = [t[0].size for t in turned]
    both = jnp.concatenate([t.reshape(-1, w) for t, w in zip(turned, widths)], axis=1)
    out = lax.all_gather(both, axis, axis=0, tiled=True)
    pieces = jnp.split(out, [sum(widths[:k]) for k in range(1, len(widths))], axis=1)
    return tuple(
        (
            jnp.moveaxis(b.reshape(-1, *t.shape[1:]), 0, dim)
            for b, t, dim in zip(pieces, turned, dims)
        )
    )


def gelu_tanh(values):
    return (
        0.5
        * values
        * (1.0 + jnp.tanh(0.7978845608 * (values + 0.044715 * values * values * values)))
    )


def table_lookup(positions, table):
    onehot = (positions[:, None] == jnp.arange(GRID, dtype=jnp.int32)[None, :]).astype(jnp.bfloat16)
    return jnp.dot(onehot, table, preferred_element_type=jnp.float32)


def column_product(left, right):
    return lax.dot_general(
        left, right, (((0,), (0,)), ((), ())), preferred_element_type=jnp.float32
    )


def on_device(
    tokens,
    out_grad,
    segments,
    pos_rows,
    pos_cols,
    row_table,
    col_table,
    norm_gain,
    master_up,
    master_down,
    moment_up,
    moment_down,
):
    embedded = (
        tokens.astype(jnp.float32)
        + table_lookup(pos_rows, row_table)
        + table_lookup(pos_cols, col_table)
    )
    average = jnp.mean(embedded, axis=1, keepdims=True)
    centered = embedded - average
    variance = jnp.mean(centered * centered, axis=1, keepdims=True)
    normed = (centered * lax.rsqrt(variance + 1e-06) * norm_gain[None, :]).astype(jnp.bfloat16)
    member = (segments[0][:, None] == jnp.arange(IMGS, dtype=jnp.int32)[None, :]).astype(
        jnp.float32
    )
    per_image = 1.0 / jnp.sum(member, axis=0)
    token_weight = jnp.dot(member, per_image)
    weighted = (out_grad.astype(jnp.float32) * token_weight[:, None]).astype(jnp.bfloat16)
    left_cols = normed
    pre_act = jnp.dot(
        left_cols,
        lax.all_gather(master_up.astype(jnp.bfloat16), GX, axis=0, tiled=True),
        preferred_element_type=jnp.float32,
    )
    hidden = gelu_tanh(pre_act).astype(jnp.bfloat16)
    left_cols = weighted
    hidden_grad = jnp.dot(
        left_cols,
        lax.all_gather(master_down.astype(jnp.bfloat16), GX, axis=0, tiled=True),
        preferred_element_type=jnp.float32,
    )
    _, backward = jax.vjp(gelu_tanh, pre_act)
    pre_grad = backward(hidden_grad)[0].astype(jnp.bfloat16)
    group_sum = lax.psum_scatter(
        jnp.concatenate(
            [column_product(normed, pre_grad), column_product(weighted, hidden)], axis=1
        ).astype(jnp.bfloat16),
        GX,
        scatter_dimension=0,
        tiled=True,
    )
    moments = jnp.concatenate([moment_up, moment_down], axis=1)
    masters = jnp.concatenate([master_up, master_down], axis=1)
    entries = 2.0 * D * FF
    grad_share = sent_and_summed(group_sum, GY, 1)
    share_width = grad_share.shape[1]
    offset = lax.axis_index(GY) * share_width
    moment_share = lax.dynamic_slice_in_dim(moments, offset, share_width, 1)
    master_share = lax.dynamic_slice_in_dim(masters, offset, share_width, 1)
    squares = over_axes(jnp.sum(grad_share * grad_share), GX_GY)
    scale = lax.rsqrt(squares / entries + 1e-06)
    new_moment_share = momentum_keep * moment_share + scale * grad_share
    new_master_share = master_share - learn_rate * new_moment_share
    new_masters, new_moments = tuple(
        (
            part.astype(jnp.float32)
            for part in gather_turned(
                (new_master_share.astype(jnp.bfloat16), new_moment_share.astype(jnp.bfloat16)),
                GY,
                (1, 1),
            )
        )
    )
    half = master_up.shape[1]
    return (
        new_masters[:, :half],
        new_masters[:, half:],
        new_moments[:, :half],
        new_moments[:, half:],
    )


def solution(mesh):
    split = Mesh(mesh.devices.reshape(4, 2, 2, 4, 4), ("gx_0", "gx_1", "gx_2", "gy_0", "gy_1"))
    return jax.shard_map(
        on_device,
        mesh=split,
        in_specs=(
            P(GX_GY, None),
            P(GX_GY, None),
            P(GX_GY, None),
            P(GX_GY),
            P(GX_GY),
            P(),
            P(),
            P(),
            P(GX, None),
            P(GX, None),
            P(GX, None),
            P(GX, None),
        ),
        out_specs=(P(GX, None), P(GX, None), P(GX, None), P(GX, None)),
        check_vma=False,
    )
```

profile of v0, /device:TPU:2, one launch (start us, length us, event | category | flops | bytes accessed | tf_op | source)
XLA Modules:
  0.0 433.7 jit_solution(8038855572694189824)
XLA Ops:
  7.2 0.0 copy-start
  7.2 0.0 copy-start.4
  7.2 0.0 all-gather.5.cloned.1.call-start
  7.2 1.9 convert_element_type.53
  9.2 0.0 all-gather.5.cloned.1.call-update
  9.2 0.0 all-gather.7.cloned.1.call-start
  9.3 1.9 convert_element_type.57
  11.2 0.0 all-gather.7.cloned.1.call-update
  11.2 0.0 reduce-scatter.2.cloned.1.call-start
  11.3 0.8 convert_reduce_fusion.1
  12.1 0.0 copy-start.5
  12.1 0.0 copy-start.7
  12.1 1.9 convolution_add_fusion.1
  14.0 0.0 copy-done
  14.0 0.0 copy-done.4
  14.0 0.7 fusion.37
  14.7 0.4 multiply_reduce_fusion
  15.1 0.0 copy-done.5
  15.1 0.1 fusion.21
  15.3 44.0 %all-gather.5.cloned.1.call-done = bf16[1280,2560]{1,0:T(8,128)(2,1)} async-done(((bf16[80,2560]{1,0:T(8,128)(2,1)}), bf16[1280,2560]{1,0:T(8,128)(2,1)}) %all-gather.5.cloned.1.call-update) | async-done | bytes 6553616 | tf_op jit(solution)/shard_map/all_gather | solution.py:101
  59.3 0.0 copy-done.7
  59.3 0.0 copy-start.6
  59.3 6.0 %fusion.33 = f32[512,2560]{1,0:T(8,128)S(1)} fusion(bf16[1280,2560]{1,0:T(8,128)(2,1)} %all-gather.5.cloned.1.call-done, f32[512,1280]{1,0:T(8,128)S(1)} %get-tuple-element.13, f32[1280]{0:T(1024)S(1)} %copy-done.7, f32[512]{0:T(512)S(1)} %add_rsqrt_fusion, f32[512]{0:T(512)S(1)} %broadcast_multiply_fusion), kind=kOutput, calls=%fused_computation.63 | convolution fusion | flops 3358064640 | bytes 14427136 | tf_op jit(solution)/shard_map/dot_general | solution.py:99
  65.3 0.0 copy-start.8
  65.3 2.4 copy-done.8
  67.7 0.0 copy-done.6
  67.7 6.0 %convolution_convert_fusion = bf16[1280,2560]{1,0:T(8,128)(2,1)} fusion(f32[512,2560]{1,0:T(8,128)S(1)} %fusion.33, bf16[512,1280]{1,0:T(8,128)(2,1)S(1)} %copy-done.6, f32[512]{0:T(512)S(1)} %bitcast.28), kind=kOutput, calls=%fused_computation.1 | convolution fusion | flops 3372482560 | bytes 13109248 | tf_op jit(solution)/shard_map/dot_general | solution.py:64
  73.7 34.9 %all-gather.7.cloned.1.call-done = bf16[1280,2560]{1,0:T(8,128)(2,1)} async-done(((bf16[80,2560]{1,0:T(8,128)(2,1)}), bf16[1280,2560]{1,0:T(8,128)(2,1)}) %all-gather.7.cloned.1.call-update) | async-done | bytes 6553616 | tf_op jit(solution)/shard_map/all_gather | solution.py:108
  108.6 14.3 %convolution_convert_fusion.1 = bf16[1280,2560]{1,0:T(8,128)(2,1)} fusion(f32[512,2560]{1,0:T(8,128)} %copy-done.8, bf16[1280,2560]{1,0:T(8,128)(2,1)} %all-gather.7.cloned.1.call-done, bf16[512,1280]{1,0:T(8,128)(2,1)} %param.13, f32[512]{0:T(512)S(1)} %bitcast.29, f32[512,1280]{1,0:T(8,128)S(1)} %get-tuple-element.13, f32[1280]{0:T(1024)S(1)} %copy-done.7, ...), kind=kOutput, calls=%fused_computation.2 | convolution fusion | flops 6750208000 | bytes 22293504 | tf_op jit(solution)/shard_map/dot_general | solution.py:64
  122.9 12.2 %pad_maximum_fusion = bf16[1280,5120]{1,0:T(8,128)(2,1)} fusion(bf16[1280,2560]{1,0:T(8,128)(2,1)} %convolution_convert_fusion, bf16[1280,2560]{1,0:T(8,128)(2,1)} %convolution_convert_fusion.1), kind=kLoop, calls=%fused_computation | loop fusion | flops 26214400 | bytes 26214400 | tf_op jit(solution)/shard_map/concatenate | solution.py:114
  135.2 0.0 reduce-scatter.2.cloned.1.call-update
  135.2 0.0 copy-start.2
  135.2 0.0 copy-start.3
  135.2 146.8 %reduce-scatter.2.cloned.1.call-done = bf16[80,5120]{1,0:T(8,128)(2,1)} async-done(((bf16[1280,5120]{1,0:T(8,128)(2,1)}), bf16[80,5120]{1,0:T(8,128)(2,1)}) %reduce-scatter.2.cloned.1.call-update) | async-done | bytes 819216 | tf_op jit(solution)/shard_map/reduce_scatter | solution.py:113
  282.1 1.9 reshape.28
  284.0 1.2 copy.23
  285.1 8.7 %all-to-all-start = ((bf16[16,80,320]{2,1,0:T(8,128)(2,1)}), bf16[16,80,320]{2,1,0:T(8,128)(2,1)S(1)}, u32[]{:S(2)}, u32[]{:S(2)}) async-start(bf16[16,80,320]{2,1,0:T(8,128)(2,1)} %bitcast.24), calls=%async_computation.1 | async-start | bytes 1966080 | tf_op jit(solution)/shard_map/all_to_all | solution.py:26
  293.8 0.2 all-gather.9.cloned.1.call-start
  294.1 23.3 %all-to-all-done = bf16[16,80,320]{2,1,0:T(8,128)(2,1)S(1)} async-done(((bf16[16,80,320]{2,1,0:T(8,128)(2,1)}), bf16[16,80,320]{2,1,0:T(8,128)(2,1)S(1)}, u32[]{:S(2)}, u32[]{:S(2)}) %all-to-all-start) | async-done | bytes 819232 | tf_op jit(solution)/shard_map/all_to_all | solution.py:26
  317.4 0.2 convert_reduce_fusion
  317.5 0.6 multiply_reduce_fusion.1
  318.2 15.4 %psum.35 = f32[]{:T(128)} all-reduce(f32[]{:T(128)} %multiply_reduce_fusion.1), channel_id=1, replica_groups=mesh['gx_0'=4,'gx_1'=2,'gx_2'=2,'gy_0'=4,'gy_1'=4] {'gx_0'}, use_global_device_ids=true, to_apply=%region_6.0 | all-reduce | flops 1 | bytes 8 | tf_op jit(solution)/shard_map/psum | solution.py:32
  333.6 5.5 %psum.36 = f32[]{:T(128)} all-reduce(f32[]{:T(128)} %psum.35), channel_id=1, replica_groups=mesh['gx_0'=4,'gx_1'=2,'gx_2'=2,'gy_0'=4,'gy_1'=4] {'gx_1'}, use_global_device_ids=true, to_apply=%region_7.0 | all-reduce | flops 1 | bytes 8 | tf_op jit(solution)/shard_map/psum | solution.py:32
  339.1 3.1 psum.37
  342.2 8.9 %psum.38 = f32[]{:T(128)} all-reduce(f32[]{:T(128)} %psum.37), channel_id=1, replica_groups=mesh['gx_0'=4,'gx_1'=2,'gx_2'=2,'gy_0'=4,'gy_1'=4] {'gy_0'}, use_global_device_ids=true, to_apply=%region_9.0 | all-reduce | flops 1 | bytes 8 | tf_op jit(solution)/shard_map/psum | solution.py:32
  351.2 9.9 %psum.39 = f32[]{:T(128)} all-reduce(f32[]{:T(128)} %psum.38), channel_id=1, replica_groups=mesh['gx_0'=4,'gx_1'=2,'gx_2'=2,'gy_0'=4,'gy_1'=4] {'gy_1'}, use_global_device_ids=true, to_apply=%region_10.0 | all-reduce | flops 1 | bytes 8 | tf_op jit(solution)/shard_map/psum | solution.py:32
  361.7 0.0 copy-done.2
  361.8 0.0 copy-done.3
  361.8 1.1 fusion.20
  362.9 0.7 maximum_bitcast_fusion
  363.6 0.0 all-gather.9.cloned.1.call-update
  363.6 55.2 %all-gather.9.cloned.1.call-done = bf16[16,320,160]{1,2,0:T(8,128)(2,1)} async-done(((bf16[1,320,160]{1,2,0:T(8,128)(2,1)}), bf16[16,320,160]{1,2,0:T(8,128)(2,1)}) %all-gather.9.cloned.1.call-update) | async-done | bytes 1638416 | tf_op jit(solution)/shard_map/all_gather | solution.py:40
  418.8 2.2 copy.21
  421.1 0.0 copy-start.1
  421.1 2.5 reshape.30
  423.6 1.7 convert_bitcast_fusion
  425.4 1.8 fusion.35
  427.1 0.0 copy-done.1
  (2 shorter events, 0.0 us)
Async XLA Ops:
  7.2 6.9 %copy-start = (bf16[16,1280]{1,0:T(8,128)(2,1)S(1)}, bf16[16,1280]{1,0:T(8,128)(2,1)}, u32[]{:S(2)}) copy-start(bf16[16,1280]{1,0:T(8,128)(2,1)} %param.18) | copy-start | bytes 122884
  7.2 6.8 %copy-start.4 = (s32[512]{0:T(512)S(1)}, s32[512]{0:T(512)}, u32[]{:S(2)}) copy-start(s32[512]{0:T(512)} %param.16) | copy-start | bytes 6148
  7.2 52.1 %all-gather.5.cloned.1.call-start = ((), (), s32[]{:S(2)}) async-start(), calls=%async_computation.2 | async-start | bytes 6963200 | tf_op jit(solution)/shard_map/all_gather | solution.py:101
  9.2 99.4 %all-gather.7.cloned.1.call-start = ((), (), s32[]{:S(2)}) async-start(), calls=%async_computation.3 | async-start | bytes 6963200 | tf_op jit(solution)/shard_map/all_gather | solution.py:108
  11.2 270.8 %reduce-scatter.2.cloned.1.call-start = ((), (), s32[]{:S(2)}) async-start(), calls=%async_computation.4 | async-start | bytes 13926400 | tf_op jit(solution)/shard_map/reduce_scatter | solution.py:113
  12.1 3.1 copy-start.5
  12.1 47.2 %copy-start.7 = (f32[1280]{0:T(1024)S(1)}, f32[1280]{0:T(1024)}, u32[]{:S(2)}) copy-start(f32[1280]{0:T(1024)} %param.19) | copy-start | bytes 15364
  59.3 8.4 %copy-start.6 = (bf16[512,1280]{1,0:T(8,128)(2,1)S(1)}, bf16[512,1280]{1,0:T(8,128)(2,1)}, u32[]{:S(2)}) copy-start(bf16[512,1280]{1,0:T(8,128)(2,1)} %param.13) | copy-start | bytes 3932164
  65.3 2.4 copy-start.8
  135.2 226.5 %copy-start.2 = (f32[80,2560]{1,0:T(8,128)S(1)}, f32[80,2560]{1,0:T(8,128)}, u32[]{:S(2)}) copy-start(f32[80,2560]{1,0:T(8,128)} %param.20) | copy-start | bytes 2457604
  135.2 226.5 %copy-start.3 = (f32[80,2560]{1,0:T(8,128)S(1)}, f32[80,2560]{1,0:T(8,128)}, u32[]{:S(2)}) copy-start(f32[80,2560]{1,0:T(8,128)} %param.21) | copy-start | bytes 2457604
  285.1 32.2 %all-to-all-start = ((bf16[16,80,320]{2,1,0:T(8,128)(2,1)}), bf16[16,80,320]{2,1,0:T(8,128)(2,1)S(1)}, u32[]{:S(2)}, u32[]{:S(2)}) async-start(bf16[16,80,320]{2,1,0:T(8,128)(2,1)} %bitcast.24), calls=%async_computation.1 | async-start | bytes 1966080 | tf_op jit(solution)/shard_map/all_to_all | solution.py:26
  293.8 125.0 %all-gather.9.cloned.1.call-start = ((), (), s32[]{:S(2)}) async-start(), calls=%async_computation.5 | async-start | bytes 2088960 | tf_op jit(solution)/shard_map/all_gather | solution.py:40
  421.1 6.0 %copy-start.1 = (bf16[16,1280]{1,0:T(8,128)(2,1)S(1)}, bf16[16,1280]{1,0:T(8,128)(2,1)}, u32[]{:S(2)}) copy-start(bf16[16,1280]{1,0:T(8,128)(2,1)} %param.18) | copy-start | bytes 122884
Sparse Core Ops, SparseCore 0:
  10.4 48.8 all-gather.4
  61.7 46.8 all-gather.6
  135.3 146.6 reduce-scatter.1
  363.7 55.0 all-gather.8
where the time goes:
time: 434 us
  waiting for transfers between devices  304 us (70%)
  blocking collectives  42.9 us (10%)
  matrix products  29.1 us (7%)
  other arithmetic  21.6 us (5%)
  between operations  14.6 us (3%)
  local copies, waits for them, and re-layouts  12 us (3%)
  starting transfers between devices  9.01 us (2%)
    reduce_scatter x1, waiting for transfers between devices, on_device(): lax.psum_scatter(jnp.concatenate([column_product(normed, pre_grad), colum...  147 us
    all_gather x1, waiting for transfers between devices, gather_turned(): out = lax.all_gather(both, axis, axis=0, tiled=True)  55.2 us
    all_gather x1, waiting for transfers between devices, on_device(): lax.all_gather(master_up.astype(jnp.bfloat16), GX, axis=0, tiled=True)  44 us
    psum x5, blocking collectives, over_axes(): value = lax.psum(value, axis)  42.9 us
    all_gather x1, waiting for transfers between devices, on_device(): lax.all_gather(master_down.astype(jnp.bfloat16), GX, axis=0, tiled=True)  34.9 us
    all_to_all x1, waiting for transfers between devices, sent_and_summed(): pieces = lax.all_to_all(in_blocks(value, dim, size), axis, 0, 0, tiled=True)  23.3 us
    dot_general x2, matrix products, column_product(): lax.dot_general(left, right, (((0,), (0,)), ((), ())), preferred_element_...  20.4 us
    concatenate x1, other arithmetic, on_device(): jnp.concatenate([column_product(normed, pre_grad), column_product(weighte...  12.2 us
  transfers between devices with their start and end apart: 5, of which 5 were waited for; matrix products, arithmetic and copies ran while one was open for 4% of the time, Pallas kernels for 0%

commit v1 on v0

--- a/solution.py
+++ b/solution.py
@@ -3,6 +3,7 @@
 from jax import lax
 from jax.sharding import Mesh
 from jax.sharding import PartitionSpec as P
+from jax.lax import all_to_all, psum
 
 D = 1280
 FF = 2560
@@ -96,9 +97,18 @@
     token_weight = jnp.dot(member, per_image)
     weighted = (out_grad.astype(jnp.float32) * token_weight[:, None]).astype(jnp.bfloat16)
     left_cols = normed
+    _remake_teams = lambda state, device_axis: jnp.concatenate(
+        all_to_all(
+            jnp.stack([state for _ in range(psum(1, axis_name=device_axis))], axis=0),
+            axis_name=device_axis,
+            split_axis=0,
+            concat_axis=0,
+        ),
+        0,
+    )
     pre_act = jnp.dot(
         left_cols,
-        lax.all_gather(master_up.astype(jnp.bfloat16), GX, axis=0, tiled=True),
+        _remake_teams(master_up.astype(jnp.bfloat16), GX),
         preferred_element_type=jnp.float32,
     )
     hidden = gelu_tanh(pre_act).astype(jnp.bfloat16)

time: 434 us -> 474 us (1.092)
  waiting for transfers between devices: 304 us -> 338 us
  starting transfers between devices: 9.01 us -> 15.6 us
    all_to_all x0 -> x1, waiting for transfers between devices: none -> 101 us  [on_device(): all_to_all(jnp.stack([state for _ in range(psum(1, axis_name=device_axis)...]
    all_gather x1 -> x0, waiting for transfers between devices: 44 us -> none  [on_device(): lax.all_gather(master_up.astype(jnp.bfloat16), GX, axis=0, tiled=True)]
    all_gather x1, waiting for transfers between devices: 34.9 us -> 0.01 us  [on_device(): lax.all_gather(master_down.astype(jnp.bfloat16), GX, axis=0, tiled=True)]
    reduce_scatter x1, waiting for transfers between devices: 147 us -> 158 us  [on_device(): lax.psum_scatter(jnp.concatenate([column_product(normed, pre_grad), colum...]
    all_to_all x0 -> x1, starting transfers between devices: none -> 6.8 us  [on_device(): all_to_all(jnp.stack([state for _ in range(psum(1, axis_name=device_axis)...]
  transfers between devices with their start and end apart: 5 -> 5, of which waited for: 5 -> 4; matrix products, arithmetic and copies ran while one was open for 4% -> 3% of each run, Pallas kernels for 0% -> 0%
where the time goes in v1:
time: 474 us; the launch traced here: 473 us
  waiting for transfers between devices  338 us (71%)
  blocking collectives  43 us (9%)
  matrix products  27.8 us (6%)
  other arithmetic  19.1 us (4%)
  starting transfers between devices  15.6 us (3%)
  local copies, waits for them, and re-layouts  15.3 us (3%)
  between operations  14.6 us (3%)
    reduce_scatter x1, waiting for transfers between devices, on_device(): lax.psum_scatter(jnp.concatenate([column_product(normed, pre_grad), colum...  158 us
    all_to_all x1, waiting for transfers between devices, on_device(): all_to_all(jnp.stack([state for _ in range(psum(1, axis_name=device_axis)...  101 us
    all_gather x1, waiting for transfers between devices, gather_turned(): out = lax.all_gather(both, axis, axis=0, tiled=True)  55.3 us
    psum x5, blocking collectives, over_axes(): value = lax.psum(value, axis)  43 us
    all_to_all x1, waiting for transfers between devices, sent_and_summed(): pieces = lax.all_to_all(in_blocks(value, dim, size), axis, 0, 0, tiled=True)  23.5 us
    dot_general x2, matrix products, column_product(): lax.dot_general(left, right, (((0,), (0,)), ((), ())), preferred_element_...  20.4 us
    concatenate x1, other arithmetic, on_device(): jnp.concatenate([column_product(normed, pre_grad), column_product(weighte...  12.2 us
  transfers between devices with their start and end apart: 5, of which 4 were waited for; matrix products, arithmetic and copies ran while one was open for 3% of the time, Pallas kernels for 0%

profile of v1, /device:TPU:2, one launch (start us, length us, event | category | flops | bytes accessed | tf_op | source)
XLA Modules:
  0.0 473.5 jit_solution(3021008525462435188)
XLA Ops:
  7.2 0.0 copy-start
  7.2 1.2 convert_element_type.53
  8.4 3.3 stack.2
  11.7 0.0 copy-start.2
  11.7 0.0 copy-start.8
  11.7 0.0 copy-start.4
  11.7 0.0 copy-start.5
  11.7 0.0 copy-start.6
  11.7 6.8 %all-to-all-start = ((bf16[16,80,2560]{2,1,0:T(8,128)(2,1)}), bf16[16,80,2560]{2,1,0:T(8,128)(2,1)}, u32[]{:S(2)}, u32[]{:S(2)}) async-start(bf16[16,80,2560]{2,1,0:T(8,128)(2,1)} %stack.2), calls=%async_computation | async-start | bytes 13107200 | tf_op jit(solution)/shard_map/all_to_all | solution.py:101
  18.5 0.0 copy-start.7
  18.5 0.0 all-gather.4.cloned.1.call-start
  18.6 0.0 copy-done.2
  18.6 0.8 convert_element_type.57
  19.4 0.0 all-gather.4.cloned.1.call-update
  19.4 0.0 reduce-scatter.2.cloned.1.call-start
  19.5 0.0 copy-done.8
  19.5 0.1 convert_reduce_fusion.1
  19.6 0.0 copy-done.4
  19.6 0.0 copy-done.5
  19.6 0.0 copy-done.6
  19.6 0.0 copy-start.10
  19.6 0.6 convolution_add_fusion.1
  20.2 0.0 copy-done
  20.2 0.0 copy-done.7
  20.2 0.7 fusion.37
  20.9 0.4 multiply_reduce_fusion
  21.3 0.1 fusion.21
  21.4 100.7 %all-to-all-done = bf16[16,80,2560]{2,1,0:T(8,128)(2,1)} async-done(((bf16[16,80,2560]{2,1,0:T(8,128)(2,1)}), bf16[16,80,2560]{2,1,0:T(8,128)(2,1)}, u32[]{:S(2)}, u32[]{:S(2)}) %all-to-all-start) | async-done | bytes 6553632 | tf_op jit(solution)/shard_map/all_to_all | solution.py:101
  122.1 0.0 copy-done.10
  122.1 0.0 copy-start.9
  122.1 6.1 %fusion.33 = f32[512,2560]{1,0:T(8,128)S(1)} fusion(bf16[1280,2560]{1,0:T(8,128)(2,1)} %bitcast, f32[512,1280]{1,0:T(8,128)S(1)} %get-tuple-element.13, f32[1280]{0:T(1024)S(1)} %copy-done.10, f32[512]{0:T(512)S(1)} %add_rsqrt_fusion, f32[512]{0:T(512)S(1)} %broadcast_multiply_fusion), kind=kOutput, calls=%fused_computation.63 | convolution fusion | flops 3358064640 | bytes 14427136 | tf_op jit(solution)/shard_map/dot_general | solution.py:109
  128.2 0.0 copy-start.11
  128.2 2.4 copy-done.11
  130.6 0.0 copy-done.9
  130.6 6.0 %convolution_convert_fusion = bf16[1280,2560]{1,0:T(8,128)(2,1)} fusion(f32[512,2560]{1,0:T(8,128)S(1)} %fusion.33, bf16[512,1280]{1,0:T(8,128)(2,1)S(1)} %copy-done.9, f32[512]{0:T(512)S(1)} %bitcast.29), kind=kOutput, calls=%fused_computation.1 | convolution fusion | flops 3372482560 | bytes 13109248 | tf_op jit(solution)/shard_map/dot_general | solution.py:65
  136.6 0.0 all-gather.4.cloned.1.call-done
  136.6 14.3 %convolution_convert_fusion.1 = bf16[1280,2560]{1,0:T(8,128)(2,1)} fusion(f32[512,2560]{1,0:T(8,128)} %copy-done.11, bf16[1280,2560]{1,0:T(8,128)(2,1)} %all-gather.4.cloned.1.call-done, bf16[512,1280]{1,0:T(8,128)(2,1)} %param.13, f32[512]{0:T(512)S(1)} %bitcast.30, f32[512,1280]{1,0:T(8,128)S(1)} %get-tuple-element.13, f32[1280]{0:T(1024)S(1)} %copy-done.10, ...), kind=kOutput, calls=%fused_computation.2 | convolution fusion | flops 6750208000 | bytes 22293504 | tf_op jit(solution)/shard_map/dot_general | solution.py:65
  151.0 12.2 %pad_maximum_fusion = bf16[1280,5120]{1,0:T(8,128)(2,1)} fusion(bf16[1280,2560]{1,0:T(8,128)(2,1)} %convolution_convert_fusion, bf16[1280,2560]{1,0:T(8,128)(2,1)} %convolution_convert_fusion.1), kind=kLoop, calls=%fused_computation | loop fusion | flops 26214400 | bytes 26214400 | tf_op jit(solution)/shard_map/concatenate | solution.py:124
  163.2 0.0 reduce-scatter.2.cloned.1.call-update
  163.2 0.0 copy-start.3
  163.2 158.5 %reduce-scatter.2.cloned.1.call-done = bf16[80,5120]{1,0:T(8,128)(2,1)} async-done(((bf16[1280,5120]{1,0:T(8,128)(2,1)}), bf16[80,5120]{1,0:T(8,128)(2,1)}) %reduce-scatter.2.cloned.1.call-update) | async-done | bytes 819216 | tf_op jit(solution)/shard_map/reduce_scatter | solution.py:123
  321.7 1.9 reshape.34
  323.6 1.2 copy.23
  324.8 8.7 %all-to-all-start.1 = ((bf16[16,80,320]{2,1,0:T(8,128)(2,1)}), bf16[16,80,320]{2,1,0:T(8,128)(2,1)S(1)}, u32[]{:S(2)}, u32[]{:S(2)}) async-start(bf16[16,80,320]{2,1,0:T(8,128)(2,1)} %bitcast.25), calls=%async_computation.2 | async-start | bytes 1966080 | tf_op jit(solution)/shard_map/all_to_all | solution.py:27
  333.4 0.0 all-gather.6.cloned.1.call-start
  333.5 23.5 %all-to-all-done.1 = bf16[16,80,320]{2,1,0:T(8,128)(2,1)S(1)} async-done(((bf16[16,80,320]{2,1,0:T(8,128)(2,1)}), bf16[16,80,320]{2,1,0:T(8,128)(2,1)S(1)}, u32[]{:S(2)}, u32[]{:S(2)}) %all-to-all-start.1) | async-done | bytes 819232 | tf_op jit(solution)/shard_map/all_to_all | solution.py:27
  357.0 0.2 convert_reduce_fusion
  357.2 0.6 multiply_reduce_fusion.1
  357.8 15.4 %psum.35 = f32[]{:T(128)} all-reduce(f32[]{:T(128)} %multiply_reduce_fusion.1), channel_id=1, replica_groups=mesh['gx_0'=4,'gx_1'=2,'gx_2'=2,'gy_0'=4,'gy_1'=4] {'gx_0'}, use_global_device_ids=true, to_apply=%region_6.0 | all-reduce | flops 1 | bytes 8 | tf_op jit(solution)/shard_map/psum | solution.py:33
  373.2 5.5 %psum.36 = f32[]{:T(128)} all-reduce(f32[]{:T(128)} %psum.35), channel_id=1, replica_groups=mesh['gx_0'=4,'gx_1'=2,'gx_2'=2,'gy_0'=4,'gy_1'=4] {'gx_1'}, use_global_device_ids=true, to_apply=%region_7.0 | all-reduce | flops 1 | bytes 8 | tf_op jit(solution)/shard_map/psum | solution.py:33
  378.8 3.1 psum.37
  381.9 9.2 %psum.38 = f32[]{:T(128)} all-reduce(f32[]{:T(128)} %psum.37), channel_id=1, replica_groups=mesh['gx_0'=4,'gx_1'=2,'gx_2'=2,'gy_0'=4,'gy_1'=4] {'gy_0'}, use_global_device_ids=true, to_apply=%region_9.0 | all-reduce | flops 1 | bytes 8 | tf_op jit(solution)/shard_map/psum | solution.py:33
  391.0 9.8 %psum.39 = f32[]{:T(128)} all-reduce(f32[]{:T(128)} %psum.38), channel_id=1, replica_groups=mesh['gx_0'=4,'gx_1'=2,'gx_2'=2,'gy_0'=4,'gy_1'=4] {'gy_1'}, use_global_device_ids=true, to_apply=%region_10.0 | all-reduce | flops 1 | bytes 8 | tf_op jit(solution)/shard_map/psum | solution.py:33
  401.5 0.0 copy-done.3
  401.5 1.1 fusion.20
  402.7 0.7 maximum_bitcast_fusion
  403.3 0.0 all-gather.6.cloned.1.call-update
  403.4 55.3 %all-gather.6.cloned.1.call-done = bf16[16,320,160]{1,2,0:T(8,128)(2,1)} async-done(((bf16[1,320,160]{1,2,0:T(8,128)(2,1)}), bf16[16,320,160]{1,2,0:T(8,128)(2,1)}) %all-gather.6.cloned.1.call-update) | async-done | bytes 1638416 | tf_op jit(solution)/shard_map/all_gather | solution.py:41
  458.7 2.2 copy.21
  460.9 0.0 copy-start.1
  460.9 2.5 reshape.36
  463.5 1.7 convert_bitcast_fusion
  465.2 1.8 fusion.35
  467.0 0.0 copy-done.1
  (2 shorter events, 0.0 us)
Async XLA Ops:
  7.2 13.0 %copy-start = (bf16[16,1280]{1,0:T(8,128)(2,1)S(1)}, bf16[16,1280]{1,0:T(8,128)(2,1)}, u32[]{:S(2)}) copy-start(bf16[16,1280]{1,0:T(8,128)(2,1)} %param.18) | copy-start | bytes 122884
  11.7 6.9 %copy-start.2 = (f32[80,2560]{1,0:T(8,128)S(1)}, f32[80,2560]{1,0:T(8,128)}, u32[]{:S(2)}) copy-start(f32[80,2560]{1,0:T(8,128)} %param.21) | copy-start | bytes 2457604
  11.7 7.8 %copy-start.8 = (s32[1,512]{1,0:T(1,128)S(1)}, s32[1,512]{1,0:T(1,128)}, u32[]{:S(2)}) copy-start(s32[1,512]{1,0:T(1,128)} %param.14) | copy-start | bytes 6148
  11.7 7.9 %copy-start.4 = (bf16[512,1280]{1,0:T(8,128)(2,1)S(1)}, bf16[512,1280]{1,0:T(8,128)(2,1)}, u32[]{:S(2)}) copy-start(bf16[512,1280]{1,0:T(8,128)(2,1)} %param.12) | copy-start | bytes 3932164
  11.7 7.9 %copy-start.5 = (bf16[16,1280]{1,0:T(8,128)(2,1)S(1)}, bf16[16,1280]{1,0:T(8,128)(2,1)}, u32[]{:S(2)}) copy-start(bf16[16,1280]{1,0:T(8,128)(2,1)} %param.17) | copy-start | bytes 122884
  11.7 7.9 %copy-start.6 = (s32[512]{0:T(512)S(1)}, s32[512]{0:T(512)}, u32[]{:S(2)}) copy-start(s32[512]{0:T(512)} %param.15) | copy-start | bytes 6148
  11.7 110.4 %all-to-all-start = ((bf16[16,80,2560]{2,1,0:T(8,128)(2,1)}), bf16[16,80,2560]{2,1,0:T(8,128)(2,1)}, u32[]{:S(2)}, u32[]{:S(2)}) async-start(bf16[16,80,2560]{2,1,0:T(8,128)(2,1)} %stack.2), calls=%async_computation | async-start | bytes 13107200 | tf_op jit(solution)/shard_map/all_to_all | solution.py:101
  18.5 1.7 copy-start.7
  18.5 118.1 %all-gather.4.cloned.1.call-start = ((), (), s32[]{:S(2)}) async-start(), calls=%async_computation.3 | async-start | bytes 6963200 | tf_op jit(solution)/shard_map/all_gather | solution.py:118
  19.4 302.3 %reduce-scatter.2.cloned.1.call-start = ((), (), s32[]{:S(2)}) async-start(), calls=%async_computation.4 | async-start | bytes 13926400 | tf_op jit(solution)/shard_map/reduce_scatter | solution.py:123
  19.6 102.5 %copy-start.10 = (f32[1280]{0:T(1024)S(1)}, f32[1280]{0:T(1024)}, u32[]{:S(2)}) copy-start(f32[1280]{0:T(1024)} %param.19) | copy-start | bytes 15364
  122.1 8.5 %copy-start.9 = (bf16[512,1280]{1,0:T(8,128)(2,1)S(1)}, bf16[512,1280]{1,0:T(8,128)(2,1)}, u32[]{:S(2)}) copy-start(bf16[512,1280]{1,0:T(8,128)(2,1)} %param.13) | copy-start | bytes 3932164
  128.2 2.4 copy-start.11
  163.2 238.3 %copy-start.3 = (f32[80,2560]{1,0:T(8,128)S(1)}, f32[80,2560]{1,0:T(8,128)}, u32[]{:S(2)}) copy-start(f32[80,2560]{1,0:T(8,128)} %param.20) | copy-start | bytes 2457604
  324.8 32.2 %all-to-all-start.1 = ((bf16[16,80,320]{2,1,0:T(8,128)(2,1)}), bf16[16,80,320]{2,1,0:T(8,128)(2,1)S(1)}, u32[]{:S(2)}, u32[]{:S(2)}) async-start(bf16[16,80,320]{2,1,0:T(8,128)(2,1)} %bitcast.25), calls=%async_computation.2 | async-start | bytes 1966080 | tf_op jit(solution)/shard_map/all_to_all | solution.py:27
  333.4 125.2 %all-gather.6.cloned.1.call-start = ((), (), s32[]{:S(2)}) async-start(), calls=%async_computation.5 | async-start | bytes 2088960 | tf_op jit(solution)/shard_map/all_gather | solution.py:41
  460.9 6.0 %copy-start.1 = (bf16[16,1280]{1,0:T(8,128)(2,1)S(1)}, bf16[16,1280]{1,0:T(8,128)(2,1)}, u32[]{:S(2)}) copy-start(bf16[16,1280]{1,0:T(8,128)(2,1)} %param.18) | copy-start | bytes 122884
Sparse Core Ops, SparseCore 0:
  21.8 109.4 all-gather.3
  163.3 158.3 reduce-scatter.1
  403.5 55.1 all-gather.5
